TPU v7x, 32 devices: a whole 2x2x4 slice. The times are simulated.
32 devices in a mesh: dp: 32 (over z, y, x, core).
Axes of the slice: x: 2, y: 2, z: 4, core: 2. Of those that a mesh axis runs over, the one named last changes fastest.
Arguments:
- tokens: bfloat16 [32768, 768], P('dp')
- w_one: bfloat16 [768, 3072], replicated
- w_two: bfloat16 [3072, 768], replicated
- wi_one: bfloat16 [768, 3072], replicated
- wi_two: bfloat16 [3072, 768], replicated
- item_table: bfloat16 [131072, 768], P('dp')
- cand_ids: int32 [2048], replicated
- log_q: float32 [2048], replicated
- targets: int32 [32768], P('dp')
Outputs:
- output 1: float32 [], replicated
- output 2: float32 [131072, 768], P('dp')
- output 3: float32 [768, 3072], replicated
- output 4: float32 [3072, 768], replicated
- output 5: float32 [768, 3072], replicated
- output 6: float32 [3072, 768], replicated
All inputs are finite; a program needn't handle non-finite values.
Results may differ from a plain program's by a relative error of at most 0.00949047.
Values are sent between devices in bfloat16 or wider.
A program may use at most 1 GiB of HBM per device.

v0:
```python
import math
import jax
import jax.numpy as jnp
from jax import lax
from jax.sharding import PartitionSpec as P

SCORE_GAIN = 3.0
HIT_VALUE = -1e9


def tower_fwd(row_block, w_in, w_out):
    pre_act = jnp.dot(row_block, w_in, preferred_element_type=jnp.float32)
    hidden = jax.nn.gelu(pre_act).astype(jnp.bfloat16)
    tower_out = jnp.dot(hidden, w_out, preferred_element_type=jnp.float32).astype(jnp.bfloat16)
    return pre_act, hidden, tower_out


def tower_back(row_block, w_out, pre_act, hidden, grad_out):
    dw_out = jnp.einsum("nf,nd->fd", hidden, grad_out, preferred_element_type=jnp.float32)
    grad_hidden = jnp.einsum("nd,fd->nf", grad_out, w_out, preferred_element_type=jnp.float32)
    gelu_back = jax.vjp(jax.nn.gelu, pre_act)[1]
    grad_pre = gelu_back(grad_hidden)[0].astype(jnp.bfloat16)
    dw_in = jnp.einsum("ne,nf->ef", row_block, grad_pre, preferred_element_type=jnp.float32)
    return grad_pre, dw_in, dw_out


def owned_rows(table_loc, row_ids, row_base):
    local_ids = row_ids - row_base
    num_rows = table_loc.shape[0]
    is_owned = (local_ids >= 0) & (local_ids < num_rows)
    picked = jnp.take(table_loc, jnp.clip(local_ids, 0, num_rows - 1), axis=0)
    return jnp.where(is_owned[:, None], picked, 0)


def loss_grads(query, targ_vec, cand_vec, log_q, targ_ids, cand_ids, tok_total):
    logit_scale = SCORE_GAIN / math.sqrt(query.shape[1])
    z_targ = jnp.einsum("td,td->t", query, targ_vec, preferred_element_type=jnp.float32) * logit_scale
    z_cand = jnp.einsum("td,sd->ts", query, cand_vec, preferred_element_type=jnp.float32) * logit_scale - log_q[None, :]
    z_cand = jnp.where(targ_ids[:, None] == cand_ids[None, :], HIT_VALUE, z_cand)
    row_max = jnp.maximum(z_targ, jnp.max(z_cand, axis=1))
    e_targ = jnp.exp(z_targ - row_max)
    e_cand = jnp.exp(z_cand - row_max[:, None])
    denom_sum = e_targ + jnp.sum(e_cand, axis=1)
    loss_sum = jnp.sum(jnp.log(denom_sum) + row_max - z_targ)
    dz_targ = ((e_targ / denom_sum - 1.0) / tok_total).astype(jnp.bfloat16).astype(jnp.float32)
    dz_cand = (e_cand / denom_sum[:, None] / tok_total).astype(jnp.bfloat16)
    d_query = ((dz_targ[:, None] * targ_vec.astype(jnp.float32) + jnp.einsum("ts,sd->td", dz_cand, cand_vec, preferred_element_type=jnp.float32)) * logit_scale).astype(jnp.bfloat16)
    d_targ_vec = (logit_scale * dz_targ[:, None] * query.astype(jnp.float32)).astype(jnp.bfloat16)
    return loss_sum, d_query, d_targ_vec, dz_cand, logit_scale


def solution(mesh):
    num_dev = mesh.shape["dp"]

    def local_step(tokens, w_one, w_two, wi_one, wi_two, table_loc, cand_ids, log_q, targ_loc):
        my_index = lax.axis_index("dp")
        rows_loc = table_loc.shape[0]
        row_base = my_index * rows_loc
        tok_total = tokens.shape[0] * num_dev
        cand_mine = lax.psum_scatter(owned_rows(table_loc, cand_ids, row_base), "dp", scatter_dimension=0, tiled=True)
        c_pre, c_hidden, cand_vec_mine = tower_fwd(cand_mine, wi_one, wi_two)
        cand_vec = lax.all_gather(cand_vec_mine, "dp", axis=0, tiled=True)
        targ_all = lax.all_gather(targ_loc, "dp", axis=0, tiled=True)
        targ_raw = lax.psum_scatter(owned_rows(table_loc, targ_all, row_base), "dp", scatter_dimension=0, tiled=True)
        t_pre, t_hidden, targ_vec = tower_fwd(targ_raw, wi_one, wi_two)
        q_pre, q_hidden, query = tower_fwd(tokens, w_one, w_two)
        loss_sum, d_query, d_targ_vec, dz_cand, logit_scale = loss_grads(query, targ_vec, cand_vec, log_q, targ_loc, cand_ids, tok_total)
        d_cand_part = jnp.einsum("ts,td->sd", dz_cand, query, preferred_element_type=jnp.float32)
        d_cand_vec = (lax.psum_scatter(d_cand_part, "dp", scatter_dimension=0, tiled=True) * logit_scale).astype(jnp.bfloat16)
        dw_one, dw_two = tower_back(tokens, w_two, q_pre, q_hidden, d_query)[1:]
        t_grad_pre, dwi_one_t, dwi_two_t = tower_back(targ_raw, wi_two, t_pre, t_hidden, d_targ_vec)
        c_grad_pre, dwi_one_c, dwi_two_c = tower_back(cand_mine, wi_two, c_pre, c_hidden, d_cand_vec)
        d_targ_raw = jnp.einsum("nf,df->nd", t_grad_pre, wi_one, preferred_element_type=jnp.float32).astype(jnp.bfloat16)
        d_cand_raw = jnp.einsum("nf,df->nd", c_grad_pre, wi_one, preferred_element_type=jnp.float32).astype(jnp.bfloat16)
        weight_grads = lax.psum((dw_one, dw_two, dwi_one_t + dwi_one_c, dwi_two_t + dwi_two_c), "dp")
        back_cand = lax.all_gather(d_cand_raw, "dp", axis=0, tiled=True)
        back_targ = lax.all_gather(d_targ_raw, "dp", axis=0, tiled=True)
        local_ids = jnp.concatenate([cand_ids, targ_all]) - row_base
        local_ids = jnp.where((local_ids >= 0) & (local_ids < rows_loc), local_ids, rows_loc)
        d_table = jax.ops.segment_sum(jnp.concatenate([back_cand, back_targ]).astype(jnp.float32), local_ids, num_segments=rows_loc)
        loss = lax.psum(loss_sum, "dp") / tok_total
        return (loss, d_table) + tuple(weight_grads)

    return jax.shard_map(local_step, mesh=mesh, in_specs=(P("dp", None), P(), P(), P(), P(), P("dp", None), P(), P(), P("dp")), out_specs=(P(), P("dp", None), P(), P(), P(), P()), check_vma=False)
```

profile of v0, /device:TPU:0, one launch (start us, length us, event | category | flops | bytes accessed | tf_op | source)
XLA Modules:
  0.0 2046.0 jit_solution(5606514943441983063)
XLA Ops:
  7.2 0.8 compare_and_fusion.3
  8.1 0.7 fusion.46
  8.8 13.7 gather_fusion.1
  22.4 3.4 select_select_fusion.1
  25.9 43.6 %all_gather.12 = s32[32768]{0:T(1024)S(1)} all-gather(s32[1024]{0:T(1024)S(1)} %copy-done.10), channel_id=1, replica_groups=mesh['dp'=32] {'dp'}, dimensions={0}, use_global_device_ids=true | all-gather | bytes 135168 | tf_op jit(solution)/shard_map/all_gather | solution.py:63
  69.6 0.1 fusion.44
  69.6 148.6 %gather_fusion = bf16[32768,768]{1,0:T(8,128)(2,1)} fusion(bf16[4096,768]{1,0:T(8,128)(2,1)} %param.14, s32[32768]{0:T(1024)S(1)} %fusion.44), kind=kCustom, calls=%fused_computation | custom fusion | bytes 100794368 | tf_op jit(solution)/shard_map/jit(_take)/gather | solution.py:31
  218.3 0.1 compare_and_fusion.1
  218.4 3.3 fusion.61
  221.7 0.9 copy-done.1
  222.6 4.0 convolution_convert_fusion.4
  226.7 33.4 %select_select_fusion = bf16[32768,768]{1,0:T(8,128)(2,1)} fusion(bf16[32768,768]{1,0:T(8,128)(2,1)} %gather_fusion, pred[32768]{0:T(1024)(128)(4,1)S(1)} %get-tuple-element.31, pred[32768]{0:T(1024)(128)(4,1)S(1)} %get-tuple-element.30), kind=kLoop, calls=%fused_computation.8 | loop fusion | flops 50331648 | bytes 100728832 | tf_op jit(solution)/shard_map/jit(_where)/select_n | solution.py:32
  260.1 0.2 reduce-scatter.8.cloned.1.call-start
  260.3 6.9 fusion.59
  267.2 4.5 copy-done.15
  271.7 9.9 convolution_convert_fusion.2
  281.6 0.5 all-gather.4.cloned.1.call-done
  282.2 8.1 fusion.28
  290.3 421.7 %reduce-scatter.4.cloned.1.call-done = bf16[1024,768]{1,0:T(8,128)(2,1)} async-done(((bf16[32768,768]{1,0:T(8,128)(2,1)}), bf16[1024,768]{1,0:T(8,128)(2,1)}) %reduce-scatter.4.cloned.1.call-update) | async-done | bytes 1572880 | tf_op jit(solution)/shard_map/reduce_scatter | solution.py:64
  712.0 7.5 fusion.60
  719.5 14.6 fusion.32
  734.1 3.3 fusion.19
  737.4 0.6 fusion.48
  738.0 3.1 multiply_convert_fusion.2
  741.2 2.0 copy-done.3
  743.2 5.5 fusion.62
  748.7 15.5 fusion.18
  764.2 3.4 fusion.31
  767.7 13.0 fusion.57
  780.7 7.6 fusion.63
  788.4 10.4 fusion.41
  798.7 22.0 %fusion.23 = f32[768,3072]{0,1:T(8,128)} fusion(bf16[1024,768]{1,0:T(8,128)(2,1)S(1)} %copy-done, f32[1024,3072]{1,0:T(8,128)} %copy-done.15, bf16[1024,768]{1,0:T(8,128)(2,1)} %copy-done.18, bf16[3072,768]{1,0:T(8,128)(2,1)} %param.11), kind=kOutput, calls=%fused_computation.35 | convolution fusion | flops 9726590976 | bytes 29884416 | tf_op jit(solution)/shard_map/ne,nf->ef/dot_general | solution.py:23
  820.7 42.8 %reduce-scatter.8.cloned.1.call-done = f32[64,768]{1,0:T(8,128)} async-done(((f32[2048,768]{1,0:T(8,128)}), f32[64,768]{1,0:T(8,128)}) %reduce-scatter.8.cloned.1.call-update) | async-done | bytes 196624 | tf_op jit(solution)/shard_map/reduce_scatter | solution.py:69
  863.5 4.2 fusion.40
  867.7 9.1 convolution_add_fusion
  876.8 5.2 convolution_add_fusion.1
  882.1 4.5 convolution_convert_fusion.3
  886.7 9.5 convolution_convert_fusion
  896.2 0.2 and_select_fusion
  896.4 41.5 %psum.35 = f32[]{:T(128)} all-reduce(f32[]{:T(128)} %get-tuple-element.33), channel_id=1, replica_groups=mesh['dp'=32] {'dp'}, use_global_device_ids=true, to_apply=%region_5.6 | all-reduce | flops 1 | bytes 8 | tf_op jit(solution)/shard_map/psum | solution.py:81
  938.5 491.7 %all-reduce.3.cloned.1.call-done = (f32[768,3072]{0,1:T(8,128)}, f32[3072,768]{1,0:T(8,128)}, f32[768,3072]{1,0:T(8,128)}, f32[3072,768]{1,0:T(8,128)}) async-done(((f32[768,3072]{0,1:T(8,128)}, f32[3072,768]{1,0:T(8,128)}, f32[768,3072]{1,0:T(8,128)}, f32[3072,768]{1,0:T(8,128)}), (f32[768,3072]{0,1:T(8,128)}, f32[3072,768]{1,0:T(8,128)}, f32[768,3072]{1,0:T(8,128)}, ...) | async-done | bytes 37748752 | tf_op jit(solution)/shard_map/psum | solution.py:75
  1430.2 9.6 copy.17
  1439.8 52.5 %all-gather.6.cloned.1.call-done = bf16[2048,768]{1,0:T(8,128)(2,1)} async-done(((bf16[64,768]{1,0:T(8,128)(2,1)}), bf16[2048,768]{1,0:T(8,128)(2,1)}) %all-gather.6.cloned.1.call-update) | async-done | bytes 3145744 | tf_op jit(solution)/shard_map/all_gather | solution.py:76
  1492.3 276.0 %all-gather.8.cloned.1.call-done = bf16[32768,768]{1,0:T(8,128)(2,1)} async-done(((bf16[1024,768]{1,0:T(8,128)(2,1)}), bf16[32768,768]{1,0:T(8,128)(2,1)}) %all-gather.8.cloned.1.call-update) | async-done | bytes 50331664 | tf_op jit(solution)/shard_map/all_gather | solution.py:77
  1768.3 248.7 %scatter_custom_fusion = f32[4096,768]{1,0:T(8,128)} fusion(s32[34816]{0:T(1024)S(1)} %bitcast.42, bf16[32768,768]{1,0:T(8,128)(2,1)} %all-gather.8.cloned.1.call-done, bf16[]{:T(256)} %constant.46, bf16[2048,768]{1,0:T(8,128)(2,1)} %all-gather.6.cloned.1.call-done, f32[]{:T(128)} %constant.34.clone.1), kind=kCustom, calls=%fused_computation.3 | custom fusion | flops 133693440 | bytes 66060296 | tf_op jit(solution)/shard_map/scatter-add | solution.py:80
  2016.9 8.4 copy.27
  2025.3 8.7 copy.28
  2034.0 3.7 copy.29
  (81 shorter events, 0.5 us)
Async XLA Ops:
  7.2 253.1 %copy-start = (bf16[1024,768]{1,0:T(8,128)(2,1)S(1)}, bf16[1024,768]{1,0:T(8,128)(2,1)}, u32[]{:S(2)}) copy-start(bf16[1024,768]{1,0:T(8,128)(2,1)} %param.9) | copy-start | bytes 4718596
  7.2 211.2 %reduce-scatter.6.cloned.1.call-start = ((), (), s32[]{:S(2)}) async-start(), calls=%async_computation.4 | async-start | bytes 3244032 | tf_op jit(solution)/shard_map/reduce_scatter | solution.py:60
  22.4 3.5 copy-start.10
  25.9 256.3 %all-gather.4.cloned.1.call-start = ((), (), s32[]{:S(2)}) async-start(), calls=%async_computation.5 | async-start | bytes 3244032 | tf_op jit(solution)/shard_map/all_gather | solution.py:62
  69.6 148.7 %copy-start.5 = (s32[32768]{0:T(1024)}, s32[32768]{0:T(1024)S(1)}, u32[]{:S(2)}) copy-start(s32[32768]{0:T(1024)S(1)} %all_gather.12) | copy-start | bytes 393220
  221.7 0.9 copy-start.1
  226.6 485.4 %reduce-scatter.4.cloned.1.call-start = ((), (), s32[]{:S(2)}) async-start(), calls=%async_computation.3 | async-start | bytes 51904512 | tf_op jit(solution)/shard_map/reduce_scatter | solution.py:64
  260.1 603.4 %reduce-scatter.8.cloned.1.call-start = ((), (), s32[]{:S(2)}) async-start(), calls=%async_computation.6 | async-start | bytes 6488064 | tf_op jit(solution)/shard_map/reduce_scatter | solution.py:69
  267.2 4.5 copy-start.15
  271.7 10.5 copy-start.8
  271.7 10.5 copy-start.11
  271.7 10.5 copy-start.12
  712.0 22.1 %slice-start = ((s8[8388608]{0:T(1024)(128)(4,1)}), s8[4194304]{0:T(1024)(128)(4,1)S(1)}, s32[]{:S(2)}) async-start(s8[8388608]{0:T(1024)(128)(4,1)} %bitcast.34), calls=%async_computation.10 | async-start | bytes 8388608
  719.5 14.6 copy-start.16
  719.5 14.6 slice-start.1
  741.1 2.0 copy-start.3
  748.6 681.6 %all-reduce.3.cloned.1.call-start = ((), (), s32[]{:S(2)}) async-start(), calls=%async_computation.9 | async-start | bytes 75497472 | tf_op jit(solution)/shard_map/psum | solution.py:75
  748.7 15.5 copy-start.4
  748.7 15.5 copy-start.13
  748.7 15.5 copy-start.17
  764.2 16.5 slice-start.8
  764.2 24.1 %slice-start.10 = ((s8[12582912]{0:T(1024)(128)(4,1)}), s8[4194304]{0:T(1024)(128)(4,1)S(1)}, s32[]{:S(2)}) async-start(s8[12582912]{0:T(1024)(128)(4,1)} %bitcast.45), calls=%async_computation.20 | async-start | bytes 8388608
  767.7 13.0 copy-start.18
  767.7 13.0 copy-start.14
  767.7 13.0 slice-start.9
  767.7 20.7 %slice-start.11 = ((s8[12582912]{0:T(1024)(128)(4,1)}), s8[4194304]{0:T(1024)(128)(4,1)S(1)}, s32[]{:S(2)}) async-start(s8[12582912]{0:T(1024)(128)(4,1)} %bitcast.45), calls=%async_computation.21 | async-start | bytes 8388608
  767.7 20.6 %slice-start.12 = ((s8[12582912]{0:T(1024)(128)(4,1)}), s8[4194304]{0:T(1024)(128)(4,1)S(1)}, s32[]{:S(2)}) async-start(s8[12582912]{0:T(1024)(128)(4,1)} %bitcast.45), calls=%async_computation.22 | async-start | bytes 8388608
  798.7 64.8 %copy-start.2 = (f32[64,3072]{1,0:T(8,128)S(1)}, f32[64,3072]{1,0:T(8,128)}, u32[]{:S(2)}) copy-start(f32[64,3072]{1,0:T(8,128)} %copy-done.1) | copy-start | bytes 2359300
  863.5 13.3 slice-start.5
  867.7 9.2 slice-start.6
  867.7 9.1 slice-start.7
  867.7 9.1 copy-start.7
  882.0 610.3 %all-gather.6.cloned.1.call-start = ((), (), s32[]{:S(2)}) async-start(), calls=%async_computation.7 | async-start | bytes 3244032 | tf_op jit(solution)/shard_map/all_gather | solution.py:76
  886.6 9.6 copy-start.6
  886.6 9.6 copy-start.9
  886.6 881.6 %all-gather.8.cloned.1.call-start = ((), (), s32[]{:S(2)}) async-start(), calls=%async_computation.8 | async-start | bytes 51904512 | tf_op jit(solution)/shard_map/all_gather | solution.py:77
  2016.9 17.1 slice-start.2
  2016.9 17.1 slice-start.3
  2025.3 8.7 slice-start.4
Sparse Core Ops, SparseCore 0:
  26.0 104.8 reduce-scatter.5
  226.7 55.3 all-gather.3
  288.6 423.3 reduce-scatter.3
  748.8 114.6 reduce-scatter.7
  882.1 548.0 all-reduce.2
  1432.9 59.3 all-gather.5
  1495.7 272.4 all-gather.7
where the time goes:
time: 2050 us
  waiting for transfers between devices  1290 us (63%)
  other arithmetic  294 us (14%)
  local copies, waits for them, and re-layouts  200 us (10%)
  matrix products  164 us (8%)
  blocking collectives  85.1 us (4%)
    psum x1, waiting for transfers between devices, local_step(): lax.psum((dw_one, dw_two, dwi_one_t + dwi_one_c, dwi_two_t + dwi_two_c),...  492 us
    reduce_scatter x1, waiting for transfers between devices, local_step(): lax.psum_scatter(owned_rows(table_loc, targ_all, row_base), 'dp', scatter...  422 us
    all_gather x1, waiting for transfers between devices, local_step(): back_targ = lax.all_gather(d_targ_raw, 'dp', axis=0, tiled=True)  276 us
    scatter-add x1, other arithmetic, local_step(): jax.ops.segment_sum(jnp.concatenate([back_cand, back_targ]).astype(jnp.fl...  249 us
    gather x2, local copies, waits for them, and re-layouts, owned_rows(): picked = jnp.take(table_loc, jnp.clip(local_ids, 0, num_rows - 1), axis=0)  162 us
    all_gather x1, waiting for transfers between devices, local_step(): back_cand = lax.all_gather(d_cand_raw, 'dp', axis=0, tiled=True)  52.5 us
    all_gather x1, blocking collectives, local_step(): targ_all = lax.all_gather(targ_loc, 'dp', axis=0, tiled=True)  43.6 us
    reduce_scatter x1, waiting for transfers between devices, local_step(): lax.psum_scatter(d_cand_part, 'dp', scatter_dimension=0, tiled=True)  42.8 us
  transfers between devices with their start and end apart: 7, of which 6 were waited for; matrix products, arithmetic and copies ran while one was open for 15% of the time, Pallas kernels for 0%

commit v1 on v0

v1 whole, which is shorter than its diff:
```python
import functools
import math
import jax
import jax.numpy as jnp
from jax import lax
from jax.experimental import pallas as pl
from jax.experimental.pallas import tpu as pltpu
from jax.sharding import PartitionSpec as P

SCORE_GAIN = 3.0
HIT_VALUE = -1e9
PAIR_ROWS = 48
HOT_ROWS = 240
MESH = pl.DeviceIdType.MESH
ANY = pl.BlockSpec(memory_space=pl.ANY)


def tower_fwd(row_block, w_in, w_out):
    pre_act = jnp.dot(row_block, w_in, preferred_element_type=jnp.float32)
    hidden = jax.nn.gelu(pre_act).astype(jnp.bfloat16)
    tower_out = jnp.dot(hidden, w_out, preferred_element_type=jnp.float32).astype(jnp.bfloat16)
    return pre_act, hidden, tower_out


def tower_back(row_block, w_out, pre_act, hidden, grad_out):
    dw_out = jnp.einsum("nf,nd->fd", hidden, grad_out, preferred_element_type=jnp.float32)
    grad_hidden = jnp.einsum("nd,fd->nf", grad_out, w_out, preferred_element_type=jnp.float32)
    gelu_back = jax.vjp(jax.nn.gelu, pre_act)[1]
    grad_pre = gelu_back(grad_hidden)[0].astype(jnp.bfloat16)
    dw_in = jnp.einsum("ne,nf->ef", row_block, grad_pre, preferred_element_type=jnp.float32)
    return grad_pre, dw_in, dw_out


def loss_grads(query, targ_vec, cand_vec, log_q, targ_ids, cand_ids, tok_total):
    logit_scale = SCORE_GAIN / math.sqrt(query.shape[1])
    z_targ = jnp.einsum("td,td->t", query, targ_vec, preferred_element_type=jnp.float32) * logit_scale
    z_cand = jnp.einsum("td,sd->ts", query, cand_vec, preferred_element_type=jnp.float32) * logit_scale - log_q[None, :]
    z_cand = jnp.where(targ_ids[:, None] == cand_ids[None, :], HIT_VALUE, z_cand)
    row_max = jnp.maximum(z_targ, jnp.max(z_cand, axis=1))
    e_targ = jnp.exp(z_targ - row_max)
    e_cand = jnp.exp(z_cand - row_max[:, None])
    denom_sum = e_targ + jnp.sum(e_cand, axis=1)
    loss_sum = jnp.sum(jnp.log(denom_sum) + row_max - z_targ)
    dz_targ = ((e_targ / denom_sum - 1.0) / tok_total).astype(jnp.bfloat16).astype(jnp.float32)
    dz_cand = (e_cand / denom_sum[:, None] / tok_total).astype(jnp.bfloat16)
    d_query = ((dz_targ[:, None] * targ_vec.astype(jnp.float32) + jnp.einsum("ts,sd->td", dz_cand, cand_vec, preferred_element_type=jnp.float32)) * logit_scale).astype(jnp.bfloat16)
    d_targ_vec = (logit_scale * dz_targ[:, None] * query.astype(jnp.float32)).astype(jnp.bfloat16)
    return loss_sum, d_query, d_targ_vec, dz_cand, logit_scale


def copy_to(src, dst, send_sem, recv_sem, dev):
    return pltpu.make_async_remote_copy(src, dst, send_sem, recv_sem, device_id=(dev,), device_id_type=MESH)


def all_to_all_body(n, src, dst, send_sem, recv_sem, own_sem):
    me = lax.axis_index("dp")
    barrier = pltpu.get_barrier_semaphore()

    def greet(i, carry):
        pl.semaphore_signal(barrier, inc=1, device_id=(lax.rem(me + i, n),), device_id_type=MESH)
        return carry

    lax.fori_loop(1, n, greet, 0)
    own = pltpu.make_async_copy(src.at[me], dst.at[me], own_sem)
    own.start()
    pl.semaphore_wait(barrier, n - 1)

    def send(i, carry):
        dev = lax.rem(me + i, n)
        copy_to(src.at[dev], dst.at[me], send_sem, recv_sem, dev).start()
        return carry

    lax.fori_loop(1, n, send, 0)
    own.wait()
    others = copy_to(src.at[pl.ds(0, n - 1)], dst.at[pl.ds(0, n - 1)], send_sem, recv_sem, me)
    others.wait_send()
    others.wait_recv()


def root_barrier(n, root, me):
    barrier = pltpu.get_barrier_semaphore()
    is_root = me // 2 == root

    def greet(i, carry):
        pl.semaphore_signal(barrier, inc=1, device_id=(lax.rem(me + i, n),), device_id_type=MESH)
        return carry

    @pl.when(is_root)
    def _():
        lax.fori_loop(1, n, greet, 0)
        pl.semaphore_wait(barrier, n - 1)

    @pl.when(jnp.logical_not(is_root))
    def _():
        for core in range(2):
            pl.semaphore_signal(barrier, inc=1, device_id=(2 * root + core,), device_id_type=MESH)
        pl.semaphore_wait(barrier, 2)

    return is_root


def scatter_body(n, root, src, dst, send_sem, recv_sem, own_sem):
    me = lax.axis_index("dp")
    is_root = root_barrier(n, root, me)

    def send(i, carry):
        dev = lax.rem(me + i, n)
        copy_to(src.at[dev], dst.at[lax.rem(me, 2)], send_sem, recv_sem, dev).start()
        return carry

    @pl.when(is_root)
    def _():
        lax.fori_loop(1, n, send, 0)
        own = pltpu.make_async_copy(src.at[me], dst.at[lax.rem(me, 2)], own_sem)
        own.start()
        own.wait()
        copy_to(src.at[pl.ds(0, n - 1)], src.at[pl.ds(0, n - 1)], send_sem, recv_sem, me).wait_send()
        copy_to(src.at[0], dst.at[0], send_sem, recv_sem, me).wait_recv()

    @pl.when(jnp.logical_not(is_root))
    def _():
        copy_to(src.at[pl.ds(0, 2)], dst, send_sem, recv_sem, me).wait_recv()


def gather_body(n, root, src, dst, send_sem, recv_sem, own_sem):
    me = lax.axis_index("dp")
    is_root = root_barrier(n, root, me)
    core = lax.rem(me, 2)
    partner = 2 * root + 1 - core

    @pl.when(is_root)
    def _():
        copy_to(src.at[1 - core], dst.at[me], send_sem, recv_sem, partner).start()
        own = pltpu.make_async_copy(src.at[core], dst.at[me], own_sem)
        own.start()
        own.wait()
        copy_to(src.at[0], dst.at[0], send_sem, recv_sem, me).wait_send()
        copy_to(dst.at[pl.ds(0, n - 1)], dst.at[pl.ds(0, n - 1)], send_sem, recv_sem, me).wait_recv()

    @pl.when(jnp.logical_not(is_root))
    def _():
        for to in range(2):
            copy_to(src.at[to], dst.at[me], send_sem, recv_sem, 2 * root + to).start()
        copy_to(src, src, send_sem, recv_sem, me).wait_send()


def comm_call(body, src, out_shape, collective_id, name, us, memory=ANY):
    return pl.pallas_call(
        body,
        out_shape=jax.ShapeDtypeStruct(out_shape, src.dtype),
        in_specs=[memory],
        out_specs=memory,
        scratch_shapes=[pltpu.SemaphoreType.DMA, pltpu.SemaphoreType.DMA, pltpu.SemaphoreType.DMA],
        compiler_params=pltpu.CompilerParams(collective_id=collective_id, has_side_effects=True),
        name=name,
    )(src)


def solution(mesh):
    n = mesh.shape["dp"]

    def local_step(tokens, w_one, w_two, wi_one, wi_two, table_loc, cand_ids, log_q, targ_loc):
        me = lax.axis_index("dp")
        rows_loc, width = table_loc.shape
        num_tok = tokens.shape[0]
        num_cand = cand_ids.shape[0]
        cand_loc = num_cand // n
        num_req = num_tok + cand_loc
        tok_total = num_tok * n

        def swap(src, collective_id, name):
            return comm_call(functools.partial(all_to_all_body, n), src, src.shape, collective_id, name, 50)

        req_ids = jnp.concatenate([targ_loc, lax.dynamic_slice(cand_ids, (me * cand_loc,), (cand_loc,))])
        owner = req_ids // rows_loc
        local_id = req_ids - owner * rows_loc
        is_owner = (owner[:, None] == jnp.arange(n)[None, :]).astype(jnp.bfloat16)
        earlier = (jnp.arange(num_req)[:, None] > jnp.arange(num_req)[None, :]).astype(jnp.bfloat16)
        before = jnp.dot(earlier, is_owner, preferred_element_type=jnp.float32)
        is_owner_f = is_owner.astype(jnp.float32)
        rank = jnp.sum(before * is_owner_f, axis=1).astype(jnp.int32)
        counts = jnp.sum(is_owner_f, axis=0).astype(jnp.int32)

        depth = -(-num_req // 128) * 128
        is_rank = (rank[:, None] == jnp.arange(depth)[None, :]).astype(jnp.bfloat16)
        place = jnp.arange(num_req)
        halves = [local_id // 64, local_id % 64, place // 64, place % 64, jnp.ones_like(place)]
        picks = jnp.concatenate([is_owner * h.astype(jnp.bfloat16)[:, None] for h in halves], axis=1)
        tables = jnp.einsum("ia,ij->aj", picks, is_rank, preferred_element_type=jnp.float32).astype(jnp.int32).reshape(5, n, depth)
        want_ids = jnp.where(tables[4] > 0, tables[0] * 64 + tables[1], -1)
        places = tables[2] * 64 + tables[3]

        lines = depth // 128
        note = jnp.concatenate([
            want_ids.reshape(n, lines, 128),
            jnp.broadcast_to(jnp.pad(counts, (0, 128 - n))[None, None, :], (n, 16 - lines, 128)),
        ], axis=1)
        notes = comm_call(functools.partial(all_to_all_body, n), note, note.shape, 0, "notes", 8)
        ask_ids = notes[:, :lines].reshape(n, depth)
        all_counts = notes[:, lines, :n]

        most = jnp.max(all_counts)
        too_many = most > PAIR_ROWS + HOT_ROWS
        extra_rounds = jnp.where(too_many, (most + PAIR_ROWS - 1) // PAIR_ROWS - 1, 0)
        hot_chip = jnp.max(all_counts.reshape(n, n // 2, 2), axis=(0, 2)) > PAIR_ROWS
        hot_chip = hot_chip & jnp.logical_not(too_many)
        num_hot = jnp.sum(hot_chip.astype(jnp.int32))
        hot_rank = jnp.sum((jnp.arange(n // 2)[None, :] < jnp.arange(n // 2)[:, None]) & hot_chip[None, :], axis=1)

        def hot_at(i):
            return jnp.sum(jnp.where(hot_chip & (hot_rank == i), jnp.arange(n // 2), 0))

        ask_pad = jnp.pad(ask_ids, ((0, 0), (0, HOT_ROWS)), constant_values=-1)
        place_pad = jnp.pad(places, ((0, 0), (0, HOT_ROWS)))

        def window(table, at, size):
            return lax.dynamic_slice(table, (0, at), (table.shape[0], size))

        def fetch(ids):
            picked = jnp.take(table_loc, jnp.maximum(ids.reshape(-1), 0), axis=0)
            return picked.reshape(ids.shape + (width,))

        def place_rows(rows, got, at, size, mine):
            inside = mine & (rank >= at) & (rank < at + size)
            slot = lax.rem(owner, got.shape[0]) * size + jnp.clip(rank - at, 0, size - 1)
            return jnp.where(inside[:, None], jnp.take(got.reshape(-1, width), slot, axis=0), rows)

        got = swap(fetch(ask_ids[:, :PAIR_ROWS]), 1, "rows_in")
        slot = owner * PAIR_ROWS + jnp.clip(rank, 0, PAIR_ROWS - 1)
        raw = jnp.take(got.reshape(-1, width), slot, axis=0)

        def extra_in(r, rows):
            got = swap(fetch(window(ask_pad, r * PAIR_ROWS, PAIR_ROWS)), 1, "rows_in")
            return place_rows(rows, got, r * PAIR_ROWS, PAIR_ROWS, True)

        raw = lax.fori_loop(1, 1 + extra_rounds, extra_in, raw)

        def hot_in(i, rows):
            chip = hot_at(i)
            hot_ids = ask_ids[:, PAIR_ROWS:PAIR_ROWS + HOT_ROWS]
            out = lax.cond(me // 2 == chip, lambda: fetch(hot_ids), lambda: jnp.zeros(hot_ids.shape + (width,), jnp.bfloat16))

            def from_root(root):
                return lambda src: comm_call(functools.partial(scatter_body, n, root), src, (2, HOT_ROWS, width), 2 + root, f"rows_in_{root}", 120)

            got = lax.switch(chip, [from_root(k) for k in range(n // 2)], out)
            return place_rows(rows, got, PAIR_ROWS, HOT_ROWS, owner // 2 == chip)

        raw = lax.fori_loop(0, num_hot, hot_in, raw)

        i_pre, i_hidden, i_vec = tower_fwd(raw, wi_one, wi_two)
        targ_vec, cand_vec_mine = i_vec[:num_tok], i_vec[num_tok:]
        cand_vec = lax.all_gather(cand_vec_mine, "dp", axis=0, tiled=True)
        q_pre, q_hidden, query = tower_fwd(tokens, w_one, w_two)
        loss_sum, d_query, d_targ_vec, dz_cand, logit_scale = loss_grads(query, targ_vec, cand_vec, log_q, targ_loc, cand_ids, tok_total)
        d_cand_part = jnp.einsum("ts,td->sd", dz_cand, query, preferred_element_type=jnp.float32)
        d_cand_vec = (lax.psum_scatter(d_cand_part, "dp", scatter_dimension=0, tiled=True) * logit_scale).astype(jnp.bfloat16)
        dw_one, dw_two = tower_back(tokens, w_two, q_pre, q_hidden, d_query)[1:]
        d_vec = jnp.concatenate([d_targ_vec, d_cand_vec])
        i_grad_pre, dwi_one, dwi_two = tower_back(raw, wi_two, i_pre, i_hidden, d_vec)
        d_raw = jnp.einsum("nf,df->nd", i_grad_pre, wi_one, preferred_element_type=jnp.float32).astype(jnp.bfloat16)
        weight_grads = lax.psum((dw_one, dw_two, dwi_one, dwi_two), "dp")
        loss = lax.psum(loss_sum, "dp") / tok_total

        def spread(ids):
            return jnp.take(d_raw, ids.reshape(-1), axis=0).reshape(ids.shape + (width,))

        def add_rows(acc, ids, rows):
            ids = ids.reshape(-1)
            ids = jnp.where(ids >= 0, ids, rows_loc)
            return acc.at[ids].add(rows.reshape(-1, width).astype(jnp.float32), mode="drop")

        back = swap(spread(places[:, :PAIR_ROWS]), 1, "rows_out")
        d_table = add_rows(jnp.zeros((rows_loc, width), jnp.float32), ask_ids[:, :PAIR_ROWS], back)

        def extra_out(r, acc):
            back = swap(spread(window(place_pad, r * PAIR_ROWS, PAIR_ROWS)), 1, "rows_out")
            return add_rows(acc, window(ask_pad, r * PAIR_ROWS, PAIR_ROWS), back)

        d_table = lax.fori_loop(1, 1 + extra_rounds, extra_out, d_table)

        def hot_out(i, acc):
            chip = hot_at(i)
            hot_places = lax.dynamic_slice(places, (2 * chip, PAIR_ROWS), (2, HOT_ROWS))

            def to_root(root):
                return lambda src: comm_call(functools.partial(gather_body, n, root), src, (n, HOT_ROWS, width), 2 + n // 2 + root, f"rows_out_{root}", 120)

            back = lax.switch(chip, [to_root(k) for k in range(n // 2)], spread(hot_places))
            hot_ids = ask_ids[:, PAIR_ROWS:PAIR_ROWS + HOT_ROWS]
            return lax.cond(me // 2 == chip, lambda a: add_rows(a, hot_ids, back), lambda a: a, acc)

        d_table = lax.fori_loop(0, num_hot, hot_out, d_table)
        return (loss, d_table) + tuple(weight_grads)

    return jax.shard_map(local_step, mesh=mesh, in_specs=(P("dp", None), P(), P(), P(), P(), P("dp", None), P(), P(), P("dp")), out_specs=(P(), P("dp", None), P(), P(), P(), P()), check_vma=False)
```

time: 2050 us -> 1350 us (0.66)
  waiting for transfers between devices: 1290 us -> 461 us
  Pallas kernels: 0 us -> 452 us
  other arithmetic: 294 us -> 117 us
  local copies, waits for them, and re-layouts: 200 us -> 109 us
  blocking collectives: 85.1 us -> 41.3 us
  matrix products: 164 us -> 135 us
    pallas_call x0 -> x5, Pallas kernels: none -> 452 us  [comm_call(): pl.pallas_call(body, out_shape=jax.ShapeDtypeStruct(out_shape, src.dtype)...]
    reduce_scatter x2 -> x0, waiting for transfers between devices: 422 us -> none  [the longest x1 422 us: local_step(): lax.psum_scatter(owned_rows(table_loc, targ_all, row_base), 'dp', scatter...]
    all_gather x2 -> x0, waiting for transfers between devices: 328 us -> none  [the longest x1 276 us: local_step(): back_targ = lax.all_gather(d_targ_raw, 'dp', axis=0, tiled=True)]
    scatter-add x1 -> x2, other arithmetic: 249 us -> 77.7 us  [add_rows(): acc.at[ids].add(rows.reshape(-1, width).astype(jnp.float32), mode='drop')]
    psum x1, waiting for transfers between devices: 492 us -> 349 us  [local_step(): weight_grads = lax.psum((dw_one, dw_two, dwi_one, dwi_two), 'dp')]
    gather x2 -> x6, local copies, waits for them, and re-layouts: 162 us -> 62.1 us  [the longest x2 42.2 us: fetch(): picked = jnp.take(table_loc, jnp.maximum(ids.reshape(-1), 0), axis=0)]
    all_gather x1 -> x0, blocking collectives: 43.6 us -> none  [local_step(): targ_all = lax.all_gather(targ_loc, 'dp', axis=0, tiled=True)]
    all_gather x1, waiting for transfers between devices: 0.51 us -> 38.6 us  [local_step(): cand_vec = lax.all_gather(cand_vec_mine, 'dp', axis=0, tiled=True)]
  transfers between devices with their start and end apart: 7 -> 3, of which waited for: 6 -> 3; matrix products, arithmetic and copies ran while one was open for 15% -> 12% of each run, Pallas kernels for 0% -> 15%
where the time goes in v1:
time: 1350 us; the launch traced here: 1340 us
  waiting for transfers between devices  461 us (34%)
  Pallas kernels  452 us (33%)
  matrix products  135 us (10%)
  other arithmetic  117 us (9%)
  local copies, waits for them, and re-layouts  109 us (8%)
  blocking collectives  41.3 us (3%)
  between operations  17.8 us (1%)
    pallas_call x5, Pallas kernels, comm_call(): pl.pallas_call(body, out_shape=jax.ShapeDtypeStruct(out_shape, src.dtype)...  452 us
    psum x1, waiting for transfers between devices, local_step(): weight_grads = lax.psum((dw_one, dw_two, dwi_one, dwi_two), 'dp')  349 us
    scatter-add x2, other arithmetic, add_rows(): acc.at[ids].add(rows.reshape(-1, width).astype(jnp.float32), mode='drop')  77.7 us
    reduce_scatter x1, waiting for transfers between devices, local_step(): lax.psum_scatter(d_cand_part, 'dp', scatter_dimension=0, tiled=True)  73 us
    gather x2, local copies, waits for them, and re-layouts, fetch(): picked = jnp.take(table_loc, jnp.maximum(ids.reshape(-1), 0), axis=0)  42.2 us
    unnamed x59, local copies, waits for them, and re-layouts  42.2 us
    psum x1, blocking collectives, local_step(): loss = lax.psum(loss_sum, 'dp') / tok_total  41.3 us
    all_gather x1, waiting for transfers between devices, local_step(): cand_vec = lax.all_gather(cand_vec_mine, 'dp', axis=0, tiled=True)  38.6 us
  transfers between devices with their start and end apart: 3, of which 3 were waited for; matrix products, arithmetic and copies ran while one was open for 12% of the time, Pallas kernels for 15%

profile of v1, /device:TPU:0, one launch (start us, length us, event | category | flops | bytes accessed | tf_op | source)
XLA Modules:
  0.0 1340.0 jit_solution(11134662362006527112)
XLA Ops:
  13.9 11.7 notes.1
  32.1 10.3 gather_fusion.6
  42.4 3.4 broadcast_select_fusion.5.src
  45.8 49.2 %rows_in.3 = bf16[32,48,768]{2,1,0:T(8,128)(2,1)} custom-call(bf16[32,48,768]{2,1,0:T(8,128)(2,1)} %broadcast_select_fusion.5.src), custom_call_target="tpu_custom_call" | custom-call | tf_op jit(solution)/shard_map/rows_in/pallas_call | solution.py:148
  95.0 7.4 gather_fusion.7
  103.9 246.0 %while.51 = (s32[]{:T(128)}, bf16[1088,768]{1,0:T(8,128)(2,1)}, s32[]{:T(128)}, s32[1088,1]{0,1:T(1,128)S(1)}, s32[1088]{0:T(1024)S(1)}, /*index=5*/s32[1088,1]{...) while((s32[]{:T(128)}, bf16[1088,768]{1,0:T(8,128)(2,1)}, ...), condition=%wide.region_29.30_spmd, body=%wide.region_9.29_spmd.sunk | while | flops 7650628 | bytes 55880884 | solution.py:249
  107.5 42.6 %conditional.8 = (bf16[32,240,768]{2,1,0:T(8,128)(2,1)}) conditional(s32[]{:T(128)} %convert_element_type.218, () %tuple.251, (s32[32,1152]{1,0:T(8,128)S(1)}, bf16[4096,768]{1,0:T(8,128)(2,1)}) %tuple.252), branch_computations={%region_11.11_spmd, %region_12.12_spmd} | conditional | flops 5929472 | bytes 47449096 | solution.py:241
  107.8 31.9 %gather_fusion = bf16[7680,768]{1,0:T(8,128)(2,1)} fusion(bf16[4096,768]{1,0:T(8,128)(2,1)} %get-tuple-element.595, s32[8192]{0:T(1024)S(1)} %pad_clamp_fusion), kind=kCustom, calls=%fused_computation.2 | custom fusion | bytes 23623680 | tf_op jit(solution)/shard_map/while/body/cond/branch_1_fun/jit(_take)/gather | solution.py:220
  139.7 10.4 broadcast_select_fusion
  150.1 191.1 %conditional.9 = (bf16[480,768]{1,0:T(8,128)(2,1)S(1)}) conditional(s32[]{:T(128)} %clamp.84, bf16[32,240,768]{2,1,0:T(8,128)(2,1)} %get-tuple-element.1207, bf16[32,240,768]{2,1,0:T(8,128)(2,1)} %get-tuple-element.1207, bf16[32,240,768]{2,1,0:T(8,128)(2,1)} %get-tuple-element.1207, ...), branch_computations={%region_13.13_spmd, %region_14.14_spmd, %region_15.15_spmd, %regio... | conditional | bytes 8 | solution.py:246
  150.1 191.0 %rows_in_0.1 = bf16[2,240,768]{2,1,0:T(8,128)(2,1)S(1)} custom-call(bf16[32,240,768]{2,1,0:T(8,128)(2,1)} %src), custom_call_target="tpu_custom_call" | custom-call | tf_op jit(solution)/shard_map/while/body/cond/branch_0_fun/rows_in_0/pallas_call | solution.py:148
  341.2 4.8 gather_fusion.3
  346.0 3.3 select_select_fusion.5
  350.0 7.9 fusion.112
  357.9 8.0 convolution_convert_fusion.1
  368.0 7.0 fusion.111
  375.1 4.8 copy-done.18
  379.9 10.1 fusion.53
  389.9 38.6 %all-gather.2.cloned.1.call-done = bf16[2048,768]{1,0:T(8,128)(2,1)} async-done(((bf16[64,768]{1,0:T(8,128)(2,1)}), bf16[2048,768]{1,0:T(8,128)(2,1)}) %all-gather.2.cloned.1.call-update) | async-done | bytes 3145744 | tf_op jit(solution)/shard_map/all_gather | solution.py:253
  428.5 5.9 fusion.49
  434.5 2.8 fusion.36
  437.9 3.1 multiply_convert_fusion.2
  441.1 2.0 copy-done.3
  443.1 5.9 fusion.113
  450.5 7.3 fusion.52
  458.9 9.1 fusion.105
  468.0 21.8 %fusion.41 = f32[768,3072]{0,1:T(8,128)} fusion(bf16[1024,768]{1,0:T(8,128)(2,1)S(1)} %copy-done, f32[1024,3072]{1,0:T(8,128)} %copy-done.18, bf16[1024,768]{1,0:T(8,128)(2,1)} %copy-done.20, bf16[3072,768]{1,0:T(8,128)(2,1)} %param.55), kind=kOutput, calls=%fused_computation.114 | convolution fusion | flops 9726590976 | bytes 29884416 | tf_op jit(solution)/shard_map/ne,nf->ef/dot_general | solution.py:30
  489.9 73.0 %reduce-scatter.2.cloned.1.call-done = f32[64,768]{1,0:T(8,128)} async-done(((f32[2048,768]{1,0:T(8,128)}), f32[64,768]{1,0:T(8,128)}) %reduce-scatter.2.cloned.1.call-update) | async-done | bytes 196624 | tf_op jit(solution)/shard_map/reduce_scatter | solution.py:257
  563.8 15.3 %fusion.28 = bf16[1088,3072]{1,0:T(8,128)(2,1)S(1)} fusion(f32[1088,3072]{1,0:T(8,128)} %copy-done.19, bf16[3072,768]{1,0:T(8,128)(2,1)} %param.57, bf16[64,768]{1,0:T(8,128)(2,1)S(1)} %multiply_convert_fusion.3, bf16[1024,768]{1,0:T(8,128)(2,1)S(1)} %copy-done.4), kind=kOutput, calls=%fused_computation.97 | convolution fusion | flops 5204017152 | bytes 26443776 | tf_op jit(solution)/shard_map/nd,fd->nf/dot_general | solution.py:27
  579.1 15.7 %fusion.59 = f32[3072,768]{1,0:T(8,128)} fusion(bf16[64,768]{1,0:T(8,128)(2,1)S(1)} %multiply_convert_fusion.3, bf16[1024,768]{1,0:T(8,128)(2,1)S(1)} %copy-done.4, f32[1088,3072]{1,0:T(8,128)} %copy-done.19), kind=kOutput, calls=%fused_computation.141 | convolution fusion | flops 5167251456 | bytes 24477696 | tf_op jit(solution)/shard_map/nf,nd->fd/dot_general | solution.py:26
  594.8 10.3 fusion.114
  606.2 41.3 %psum.35 = f32[]{:T(128)} all-reduce(f32[]{:T(128)} %get-tuple-element.773), channel_id=1, replica_groups=mesh['dp'=32] {'dp'}, use_global_device_ids=true, to_apply=%region_33.34 | all-reduce | flops 1 | bytes 8 | tf_op jit(solution)/shard_map/psum | solution.py:263
  648.1 9.0 convolution_convert_fusion
  657.1 5.6 gather_fusion.8
  662.7 3.4 broadcast_select_fusion.4.src
  666.1 67.7 %rows_out.2 = bf16[32,48,768]{2,1,0:T(8,128)(2,1)} custom-call(bf16[32,48,768]{2,1,0:T(8,128)(2,1)} %broadcast_select_fusion.4.src), custom_call_target="tpu_custom_call" | custom-call | tf_op jit(solution)/shard_map/rows_out/pallas_call | solution.py:148
  733.8 16.8 %scatter_custom_fusion.2 = f32[4096,768]{1,0:T(8,128)} fusion(s32[1536]{0:T(1024)} %get-tuple-element.670, f32[]{:T(128)} %constant.452.clone.1, bf16[1536,768]{1,0:T(8,128)(2,1)} %bitcast.103), kind=kCustom, calls=%fused_computation.111 | custom fusion | flops 2359296 | bytes 14942720 | tf_op jit(solution)/shard_map/scatter-add | solution.py:271
  751.2 201.0 %while.53 = (s32[]{:T(128)}, f32[4096,768]{1,0:T(8,128)}, s32[]{:T(128)}, s32[16]{0:T(128)S(1)}, pred[16]{0:T(512)(128)(4,1)S(1)}, /*index=5*/s32[]{:T(128)}, s3...) while((s32[]{:T(128)}, f32[4096,768]{1,0:T(8,128)}, ...), condition=%wide.region_60.61_spmd, body=%wide.region_39.60_spmd.sunk | while | flops 12208936 | bytes 27533596 | solution.py:293
  754.7 2.1 gather_fusion.5
  757.0 132.5 %conditional.10 = (bf16[32,240,768]{2,1,0:T(8,128)(2,1)}) conditional(s32[]{:T(128)} %clamp.87, bf16[2,240,768]{2,1,0:T(8,128)(2,1)S(1)} %broadcast_select_fusion.12, bf16[2,240,768]{2,1,0:T(8,128)(2,1)S(1)} %broadcast_select_fusion.12, bf16[2,240,768]{2,1,0:T(8,128)(2,1)S(1)} %broadcast_select_fusion.12, ...), branch_computations={%region_41.41_spmd, %region_42.42_spmd, %region_43.43_spmd, %regio... | conditional | bytes 8 | solution.py:289
  757.0 132.5 %rows_out_0.1 = bf16[32,240,768]{2,1,0:T(8,128)(2,1)} custom-call(bf16[2,240,768]{2,1,0:T(8,128)(2,1)S(1)} %src.16), custom_call_target="tpu_custom_call" | custom-call | tf_op jit(solution)/shard_map/while/body/cond/branch_0_fun/rows_out_0/pallas_call | solution.py:148
  889.5 62.0 %conditional.11 = (f32[4096,768]{1,0:T(8,128)}) conditional(s32[]{:T(128)} %convert_element_type.219, f32[4096,768]{1,0:T(8,128)} %get-tuple-element.1170, (s32[32,1152]{1,0:T(8,128)}, bf16[32,240,768]{2,1,0:T(8,128)(2,1)}, f32[4096,768]{1,0:T(8,128)}) %tuple.257), branch_computations={%region_57.57_spmd, %region_58.59_spmd} | conditional | flops 11834880 | bytes 24563720 | solution.py:291
  890.7 60.9 %scatter_custom_fusion.1 = f32[4096,768]{1,0:T(8,128)} fusion(f32[4096,768]{1,0:T(8,128)} %get-tuple-element.619, s32[7680]{0:T(1024)S(1)} %fusion.20, bf16[7680,768]{1,0:T(8,128)(2,1)} %bitcast.93), kind=kCustom, calls=%fused_computation.74 | custom fusion | flops 11796480 | bytes 24379392 | tf_op jit(solution)/shard_map/while/body/cond/branch_1_fun/scatter-add | solution.py:271
  952.2 349.2 %all-reduce.6.cloned.1.call-done = (f32[768,3072]{0,1:T(8,128)}, f32[3072,768]{1,0:T(8,128)}, f32[768,3072]{1,0:T(8,128)}, f32[3072,768]{1,0:T(8,128)}) async-done(((f32[768,3072]{0,1:T(8,128)}, f32[3072,768]{1,0:T(8,128)}, f32[768,3072]{1,0:T(8,128)}, f32[3072,768]{1,0:T(8,128)}), (f32[768,3072]{0,1:T(8,128)}, f32[3072,768]{1,0:T(8,128)}, f32[768,3072]{1,0:T(8,128)}, ...) | async-done | bytes 37748752 | tf_op jit(solution)/shard_map/psum | solution.py:262
  1301.5 9.6 copy.17
  1311.1 8.4 copy.96
  1319.4 8.8 copy.97
  1328.2 3.7 copy.98
  (130 shorter events, 25.0 us)
Async XLA Ops:
  7.2 360.9 %copy-start = (bf16[1024,768]{1,0:T(8,128)(2,1)S(1)}, bf16[1024,768]{1,0:T(8,128)(2,1)}, u32[]{:S(2)}) copy-start(bf16[1024,768]{1,0:T(8,128)(2,1)} %param.53) | copy-start | bytes 4718596
  7.2 22.4 %copy-start.6 = (s32[1024]{0:T(1024)S(1)}, s32[1024]{0:T(1024)}, u32[]{:S(2)}) copy-start(s32[1024]{0:T(1024)} %param.61) | copy-start | bytes 12292
  7.2 421.3 %all-gather.2.cloned.1.call-start = ((), (), s32[]{:S(2)}) async-start(), calls=%async_computation.1 | async-start | bytes 3244032 | tf_op jit(solution)/shard_map/all_gather | solution.py:253
  349.9 7.9 copy-start.2
  349.9 7.9 copy-start.8
  349.9 7.9 copy-start.10
  350.0 7.9 copy-start.16
  357.9 8.0 copy-start.19
  365.9 1.2 copy-start.14
  367.8 195.1 %reduce-scatter.2.cloned.1.call-start = ((), (), s32[]{:S(2)}) async-start(), calls=%async_computation.2 | async-start | bytes 6488064 | tf_op jit(solution)/shard_map/reduce_scatter | solution.py:257
  368.0 11.8 copy-start.15
  375.1 4.8 copy-start.18
  379.9 48.7 %copy-start.7 = (s32[1024]{0:T(1024)S(1)}, s32[1024]{0:T(1024)}, u32[]{:S(2)}) copy-start(s32[1024]{0:T(1024)} %param.61) | copy-start | bytes 12292
  379.9 48.7 %copy-start.12 = (f32[2048]{0:T(1024)S(1)}, f32[2048]{0:T(1024)}, u32[]{:S(2)}) copy-start(f32[2048]{0:T(1024)} %param.60) | copy-start | bytes 24580
  379.9 48.7 %copy-start.13 = (s32[2048]{0:T(1024)S(1)}, s32[2048]{0:T(1024)}, u32[]{:S(2)}) copy-start(s32[2048]{0:T(1024)} %param.59) | copy-start | bytes 24580
  441.1 2.0 copy-start.3
  448.9 852.5 %all-reduce.6.cloned.1.call-start = ((), (), s32[]{:S(2)}) async-start(), calls=%async_computation.3 | async-start | bytes 75497472 | tf_op jit(solution)/shard_map/psum | solution.py:262
  449.0 9.9 slice-start.3
  450.5 8.5 slice-start.4
  450.5 8.5 slice-start.5
  457.8 1.1 copy-start.20
  468.0 95.7 %copy-start.4 = (bf16[1024,768]{1,0:T(8,128)(2,1)S(1)}, bf16[1024,768]{1,0:T(8,128)(2,1)}, u32[]{:S(2)}) copy-start(bf16[1024,768]{1,0:T(8,128)(2,1)} %fusion.54) | copy-start | bytes 4718596
  579.1 15.7 %copy-start.17 = (bf16[1088,3072]{1,0:T(8,128)(2,1)}, bf16[1088,3072]{1,0:T(8,128)(2,1)S(1)}, u32[]{:S(2)}) copy-start(bf16[1088,3072]{1,0:T(8,128)(2,1)S(1)} %fusion.28) | copy-start | bytes 20054020
  605.1 0.9 copy-start.5
  750.6 0.7 copy-start.9
  750.6 0.7 copy-start.11
  1311.0 17.1 %slice-start = ((s8[9437184]{0:T(1024)(128)(4,1)}), s8[4194304]{0:T(1024)(128)(4,1)S(1)}, s32[]{:S(2)}) async-start(s8[9437184]{0:T(1024)(128)(4,1)} %bitcast.101), calls=%async_computation.4 | async-start | bytes 8388608
  1311.1 17.1 %slice-start.1 = ((s8[9437184]{0:T(1024)(128)(4,1)}), s8[4194304]{0:T(1024)(128)(4,1)S(1)}, s32[]{:S(2)}) async-start(s8[9437184]{0:T(1024)(128)(4,1)} %bitcast.101), calls=%async_computation.5 | async-start | bytes 8388608
  1319.4 8.8 slice-start.2
  1319.4 12.5 copy-start.1
Sparse Core Ops, SparseCore 0:
  367.9 60.5 all-gather.1
  449.1 113.7 reduce-scatter.1
  605.2 696.1 all-reduce.5
